TPU v7x, 32 devices: a whole 2x2x4 slice. The times are simulated.
32 devices in a mesh: tp: 8 (over z, y), kv: 4 (over x, core).
Axes of the slice: x: 2, y: 2, z: 4, core: 2. Of those that a mesh axis runs over, the one named last changes fastest.
Arguments:
- hidden_in: bfloat16 [2048, 4096], P(('kv', 'tp')), may hold values from -6 to 6
- gain_attn: float32 [4096], replicated, may hold values from 0.4 to 1.6
- w_qkv: bfloat16 [4096, 32, 384], P(None, 'tp'), may hold values from -0.09375 to 0.09375
- cache_kv: bfloat16 [2, 8192, 32, 256], P(None, 'kv', 'tp'), may hold values from -110 to 110
- cache_len: int32 [2], replicated, may hold values from 128 to 8192, as said below
- w_out: bfloat16 [4096, 4096], P('tp'), may hold values from -0.1875 to 0.1875
- gain_mlp: float32 [4096], replicated, may hold values from 0.1 to 1.9
- w_gate_up: bfloat16 [4096, 2, 11008], P('kv', None, 'tp'), may hold values from -0.09375 to 0.09375
- w_down: bfloat16 [11008, 4096], P('tp', 'kv'), may hold values from -0.0546875 to 0.0546875
Outputs:
- layer_out: bfloat16 [2048, 4096], P(('kv', 'tp'))
Inputs may be any that keep to these rules, and one draw needn't show every extreme that they name: `cache_len`: every length is a multiple of 128; some sequence uses the whole cache.
All inputs are finite; a program needn't handle non-finite values.
Results may differ from a plain program's by a relative error of at most 0.019.
The roundings to bfloat16 on the way count: a program that leaves them out, or rounds other values in their place, can miss the bound.
Values may be sent and summed in bfloat16 or wider, within the bound.
A program may use at most 192 MiB of HBM per device.

v0:
```python
import math
import jax
import jax.numpy as jnp
from jax import lax
from jax.sharding import PartitionSpec as P

EPSILON = 1e-05
MASKED = -1e30


def rms_scale(values_in, gain_vector):
    widened = values_in.astype(jnp.float32)
    mean_square = jnp.mean(widened * widened, axis=-1, keepdims=True)
    return (widened * lax.rsqrt(mean_square + EPSILON) * gain_vector).astype(jnp.bfloat16)


def per_device(
    hidden_in, gain_attn, w_qkv, cache_kv, cache_len, w_out, gain_mlp, w_gate_up, w_down
):
    local_heads = w_qkv.shape[1]
    head_dim = w_qkv.shape[2] // 3
    own_rows = hidden_in.shape[0]
    block_input = lax.all_gather(hidden_in, "tp", axis=0, tiled=True)
    block_rows = block_input.shape[0]
    normed = rms_scale(block_input, gain_attn)
    flat_qkv = w_qkv.reshape(w_qkv.shape[0], local_heads * 3 * head_dim)
    packed = jnp.dot(normed, flat_qkv, preferred_element_type=jnp.float32).astype(jnp.bfloat16)
    packed = packed.reshape(block_rows, local_heads, 3 * head_dim)
    key_mine = packed[:, :, head_dim : 2 * head_dim]
    value_mine = packed[:, :, 2 * head_dim :]
    query_rows = lax.all_gather(packed[:, :, :head_dim], "kv", axis=0, tiled=True)
    seq_count = cache_kv.shape[0]
    span_len = query_rows.shape[0] // seq_count
    kv_index = lax.axis_index("kv")
    cache_rows = cache_kv.shape[1]
    cache_pos = kv_index * cache_rows + jnp.arange(cache_rows, dtype=jnp.int32)
    own_seq = (kv_index * block_rows + jnp.arange(block_rows, dtype=jnp.int32)) // span_len
    row_peaks, masses, accums = ([], [], [])
    for seq_id in range(seq_count):
        query_block = query_rows[seq_id * span_len : (seq_id + 1) * span_len]
        joined_key_rows = jnp.concatenate([cache_kv[seq_id, :, :, :head_dim], key_mine], axis=0)
        joined_value_rows = jnp.concatenate([cache_kv[seq_id, :, :, head_dim:], value_mine], axis=0)
        usable = jnp.concatenate([cache_pos < cache_len[seq_id], own_seq == seq_id])
        logit_scores = jnp.einsum(
            "qhd,khd->hqk", query_block, joined_key_rows, preferred_element_type=jnp.float32
        ) / math.sqrt(head_dim)
        logit_scores = jnp.where(usable[None, None, :], logit_scores, MASKED)
        row_peak = jnp.max(logit_scores, axis=2)
        raw_weights = jnp.where(
            usable[None, None, :], jnp.exp(logit_scores - row_peak[:, :, None]), 0.0
        )
        row_peaks.append(row_peak.T)
        masses.append(jnp.sum(raw_weights, axis=2).T)
        accums.append(
            jnp.einsum(
                "hqk,khd->qhd",
                raw_weights.astype(jnp.bfloat16),
                joined_value_rows,
                preferred_element_type=jnp.float32,
            )
        )
    peak_all = jnp.concatenate(row_peaks, axis=0)
    mass_all = jnp.concatenate(masses, axis=0)
    accum_all = jnp.concatenate(accums, axis=0)
    peak_set, mass_set, accum_set = (
        lax.all_to_all(peak_all[None], "kv", split_axis=1, concat_axis=0, tiled=True),
        lax.all_to_all(mass_all[None], "kv", split_axis=1, concat_axis=0, tiled=True),
        lax.all_to_all(accum_all[None], "kv", split_axis=1, concat_axis=0, tiled=True),
    )
    peak_best = jnp.max(peak_set, axis=0)
    scaling = jnp.exp(peak_set - peak_best[None])
    mass_own = jnp.sum(mass_set * scaling, axis=0)
    accum_own = jnp.sum(accum_set * scaling[..., None], axis=0)
    attended = (
        (accum_own / mass_own[..., None])
        .astype(jnp.bfloat16)
        .reshape(block_rows, local_heads * head_dim)
    )
    tp_index = lax.axis_index("tp")
    heads_sum = lax.psum(
        jnp.dot(attended, w_out, preferred_element_type=jnp.float32).astype(jnp.bfloat16), "tp"
    ).astype(jnp.float32)
    residual = block_input.astype(jnp.float32) + heads_sum
    mlp_in = rms_scale(residual, gain_mlp)
    residual_own = lax.dynamic_slice_in_dim(residual, tp_index * own_rows, own_rows, 0)
    gate_up = jnp.einsum(
        "td,dgf->tgf",
        mlp_in,
        lax.all_gather(w_gate_up, "kv", axis=0, tiled=True),
        preferred_element_type=jnp.float32,
    )
    activated = (jax.nn.silu(gate_up[:, 0, :]) * gate_up[:, 1, :]).astype(jnp.bfloat16)
    down_terms = jnp.dot(
        activated,
        lax.all_gather(w_down, "kv", axis=1, tiled=True),
        preferred_element_type=jnp.float32,
    )
    down_own = lax.psum_scatter(
        down_terms.astype(jnp.bfloat16), "tp", scatter_dimension=0, tiled=True
    ).astype(jnp.float32)
    return (residual_own + down_own).astype(jnp.bfloat16)


def solution(mesh):
    in_specs = (
        P(("kv", "tp"), None),
        P(),
        P(None, "tp", None),
        P(None, "kv", "tp", None),
        P(),
        P("tp", None),
        P(),
        P("kv", None, "tp"),
        P("tp", "kv"),
    )
    out_specs = P(("kv", "tp"), None)
    return jax.shard_map(
        per_device, mesh=mesh, in_specs=in_specs, out_specs=out_specs, check_vma=False
    )
```

profile of v0, /device:TPU:0, one launch (start us, length us, event | category | flops | bytes accessed | tf_op | source)
XLA Modules:
  0.0 827.3 jit_solution(16002876231132787441)
XLA Ops:
  6.5 0.7 all-gather.5.cloned.1.call-update
  7.3 12.4 %copy.51 = bf16[512,8,4,384]{3,1,2,0:T(8,128)(2,1)} copy(bf16[512,8,4,384]{3,2,1,0:T(4,128)(2,1)} %bitcast.50) | data formatting | bytes 25165824
  19.7 65.3 %all-gather.5.cloned.1.call-done = bf16[512,4096]{1,0:T(8,128)(2,1)} async-done(((bf16[64,4096]{1,0:T(8,128)(2,1)}), bf16[512,4096]{1,0:T(8,128)(2,1)}) %all-gather.5.cloned.1.call-update) | async-done | bytes 4194320 | tf_op jit(solution)/shard_map/all_gather | solution.py:23
  85.0 3.1 fusion.12
  88.1 11.0 %fusion.24 = bf16[512,1536]{1,0:T(8,128)(2,1)S(1)} fusion(bf16[4096,1536]{1,0:T(8,128)(2,1)} %bitcast.51, bf16[512,4096]{1,0:T(8,128)(2,1)} %all-gather.5.cloned.1.call-done, f32[4096]{0:T(1024)S(1)} %copy-done.5, f32[512]{0:T(512)S(1)} %add_rsqrt_fusion.1), kind=kOutput, calls=%fused_computation.37 | convolution fusion | flops 6451625984 | bytes 18368512 | tf_op jit(solution)/shard_map/dot_general | solution.py:27
  99.5 0.5 fusion.62
  100.0 0.9 copy.46
  100.9 6.4 fusion.61
  107.4 4.4 copy.44
  111.8 2.6 copy.49
  114.4 0.6 fusion.63
  115.0 1.3 fusion.45
  116.3 4.1 copy_bitcast_fusion
  120.4 1.1 copy.45
  121.6 0.6 all-gather.7.cloned.1.call-done
  122.2 19.7 %fusion.1 = (f32[4,1024]{1,0:T(4,128)S(1)}, f32[4,1024,2560]{2,1,0:T(8,128)}) fusion(pred[2560]{0:T(1024)(128)(4,1)S(1)} %pad_add_fusion.1, bf16[512,4,128]{2,0,1:T(8,128)(2,1)S(1)} %copy.48, bf16[2048,4,128]{2,0,1:T(8,128)(2,1)} %get-tuple-element.26, bf16[2048,4,128]{2,0,1:T(8,128)(2,1)} %all-gather.7.cloned.1.call-done), kind=kOutput, calls=%fused_computation.5 | convolution fusion | flops 2721050624 | bytes 45632000 | tf_op jit(solution)/shard_map/qhd,khd->hqk/dot_general | solution.py:44
  141.8 19.2 %fusion.4 = f32[4,1024]{1,0:T(4,128)S(1)} fusion(f32[4,1024,2560]{2,1,0:T(8,128)} %get-tuple-element.19, f32[4,1024]{1,0:T(4,128)S(1)} %get-tuple-element.18, pred[2560]{0:T(1024)(128)(4,1)S(1)} %pad_add_fusion.1), kind=kLoop, calls=%fused_computation.8 | loop fusion | flops 52424704 | bytes 41978368 | tf_op jit(solution)/shard_map/reduce_sum | solution.py:53
  161.1 17.9 %fusion.38 = f32[1024,4,128]{0,2,1:T(8,128)} fusion(f32[4,1024,2560]{2,1,0:T(8,128)} %get-tuple-element.19, f32[4,1024]{1,0:T(4,128)S(1)} %get-tuple-element.18, pred[2560]{0:T(1024)(128)(4,1)S(1)} %pad_add_fusion.1, bf16[512,4,128]{0,2,1:T(8,128)(2,1)S(1)} %copy-done.3, bf16[2048,4,128]{0,2,1:T(8,128)(2,1)S(1)} %bitcast.59), kind=kOutput, calls=%fused_computation.51 | convolution fusion | flops 2742026240 | bytes 46680576 | tf_op jit(solution)/shard_map/hqk,khd->qhd/dot_general | solution.py:55
  178.9 19.0 %fusion = (f32[4,1024]{1,0:T(4,128)S(1)}, f32[4,1024,2560]{2,1,0:T(8,128)}) fusion(pred[2560]{0:T(1024)(128)(4,1)S(1)} %pad_add_fusion, bf16[512,4,128]{2,0,1:T(8,128)(2,1)S(1)} %copy.48, bf16[2048,4,128]{2,0,1:T(8,128)(2,1)S(1)} %get-tuple-element.27, bf16[2048,4,128]{2,0,1:T(8,128)(2,1)} %all-gather.7.cloned.1.call-done), kind=kOutput, calls=%fused_computation.4 | convolution fusion | flops 2721050624 | bytes 45632000 | tf_op jit(solution)/shard_map/qhd,khd->hqk/dot_general | solution.py:44
  198.0 19.2 %fusion.2 = f32[4,1024]{1,0:T(4,128)S(1)} fusion(f32[4,1024,2560]{2,1,0:T(8,128)} %get-tuple-element.21, f32[4,1024]{1,0:T(4,128)S(1)} %get-tuple-element.20, pred[2560]{0:T(1024)(128)(4,1)S(1)} %pad_add_fusion), kind=kLoop, calls=%fused_computation.6 | loop fusion | flops 52424704 | bytes 41978368 | tf_op jit(solution)/shard_map/reduce_sum | solution.py:53
  217.2 17.9 %fusion.35 = f32[1024,4,128]{0,2,1:T(8,128)} fusion(f32[4,1024,2560]{2,1,0:T(8,128)} %get-tuple-element.21, f32[4,1024]{1,0:T(4,128)S(1)} %get-tuple-element.20, pred[2560]{0:T(1024)(128)(4,1)S(1)} %pad_add_fusion, bf16[512,4,128]{0,2,1:T(8,128)(2,1)S(1)} %copy-done.3, bf16[2048,4,128]{0,2,1:T(8,128)(2,1)S(1)} %bitcast.58), kind=kOutput, calls=%fused_computation.50 | convolution fusion | flops 2742026240 | bytes 46680576 | tf_op jit(solution)/shard_map/hqk,khd->qhd/dot_general | solution.py:55
  235.5 0.6 broadcast.98
  236.1 9.5 %reduce.2 = f32[2048,4]{1,0:T(8,128)S(1)} reduce(f32[2048,1,4]{2,1,0:T(1,128)S(1)} %bitcast.54, f32[]{:T(128)} %broadcast.98), dimensions={1}, to_apply=%bitcast.41.reduce_sub_computation | reduce | bytes 65540
  245.6 1.3 reshape.59
  247.0 3.3 all-to-all-start.1
  250.6 9.3 %reduce = f32[2048,4]{1,0:T(8,128)S(1)} reduce(f32[2048,1,4]{2,1,0:T(1,128)S(1)} %bitcast.55, f32[]{:T(128)} %broadcast.98), dimensions={1}, to_apply=%bitcast.43.reduce_sub_computation | reduce | bytes 65540
  260.0 1.4 reshape.61
  261.3 3.3 all-to-all-start.2
  264.6 4.6 maximum_bitcast_fusion
  269.2 5.2 copy.37
  274.5 4.9 all-to-all-start
  279.8 0.7 reduce.3
  280.5 1.7 reshape.60
  282.7 0.7 reduce.1
  283.5 1.7 reshape.62
  285.5 42.0 %all-to-all-done = f32[1,2048,4,128]{3,2,0,1:T(4,128)} async-done(((f32[1,2048,4,128]{3,2,0,1:T(4,128)}), f32[1,2048,4,128]{3,2,0,1:T(4,128)}, u32[]{:S(2)}, u32[]{:S(2)}) %all-to-all-start) | async-done | bytes 4194336 | tf_op jit(solution)/shard_map/all_to_all | solution.py:68
  327.5 5.3 copy.41
  332.9 5.1 multiply_reduce_fusion.1
  338.1 4.5 convolution_convert_fusion.1
  343.3 0.5 all-gather.11.cloned.1.call-update
  344.1 155.1 %all-reduce.2.cloned.1.call-done = bf16[512,4096]{1,0:T(8,128)(2,1)} async-done(((bf16[512,4096]{1,0:T(8,128)(2,1)}), bf16[512,4096]{1,0:T(8,128)(2,1)}) %all-reduce.2.cloned.1.call-update) | async-done | bytes 4194320 | tf_op jit(solution)/shard_map/psum | solution.py:80
  499.2 9.2 %convert_add_fusion = (f32[512,4096]{1,0:T(8,128)}, f32[512]{0:T(512)S(1)}) fusion(bf16[512,4096]{1,0:T(8,128)(2,1)} %all-gather.5.cloned.1.call-done, bf16[512,4096]{1,0:T(8,128)(2,1)} %all-reduce.2.cloned.1.call-done), kind=kLoop, calls=%fused_computation.14 | loop fusion | flops 10485248 | bytes 16779264 | tf_op jit(solution)/shard_map/add | solution.py:83
  508.4 131.6 %all-gather.9.cloned.1.call-done = bf16[4096,2,1376]{0,2,1:T(8,128)(2,1)} async-done(((bf16[1024,2,1376]{0,2,1:T(8,128)(2,1)}), bf16[4096,2,1376]{0,2,1:T(8,128)(2,1)}) %all-gather.9.cloned.1.call-update) | async-done | bytes 22544400 | tf_op jit(solution)/shard_map/all_gather | solution.py:89
  639.9 20.5 %fusion.16 = f32[512,2,1376]{0,2,1:T(8,128)} fusion(bf16[4096,2,1376]{0,2,1:T(8,128)(2,1)} %all-gather.9.cloned.1.call-done, f32[4096]{0:T(1024)S(1)} %copy-done.6, f32[512]{0:T(512)S(1)} %add_rsqrt_fusion, bf16[512,4096]{1,0:T(8,128)(2,1)} %all-gather.5.cloned.1.call-done, bf16[512,4096]{1,0:T(8,128)(2,1)} %all-reduce.2.cloned.1.call-done), kind=kOutput, calls=%fused_computation.25 | convolution fusion | flops 11555307520 | bytes 36587520 | tf_op jit(solution)/shard_map/td,dgf->tgf/dot_general | solution.py:86
  660.4 55.6 %all-gather.11.cloned.1.call-done = bf16[1376,4096]{1,0:T(8,128)(2,1)} async-done(((bf16[1376,1024]{1,0:T(8,128)(2,1)}), bf16[1376,4096]{1,0:T(8,128)(2,1)}) %all-gather.11.cloned.1.call-update) | async-done | bytes 11272208 | tf_op jit(solution)/shard_map/all_gather | solution.py:95
  716.0 13.6 %convolution_convert_fusion = bf16[512,4096]{1,0:T(8,128)(2,1)} fusion(bf16[1376,4096]{1,0:T(8,128)(2,1)} %all-gather.11.cloned.1.call-done, f32[512,2,1376]{0,2,1:T(8,128)} %fusion.16), kind=kOutput, calls=%fused_computation.22 | convolution fusion | flops 5777686528 | bytes 21102592 | tf_op jit(solution)/shard_map/dot_general | solution.py:93
  729.6 88.4 %reduce-scatter.2.cloned.1.call-done = bf16[64,4096]{1,0:T(8,128)(2,1)} async-done(((bf16[512,4096]{1,0:T(8,128)(2,1)}), bf16[64,4096]{1,0:T(8,128)(2,1)}) %reduce-scatter.2.cloned.1.call-update) | async-done | bytes 524304 | tf_op jit(solution)/shard_map/reduce_scatter | solution.py:98
  818.0 2.3 add_convert_fusion
  (43 shorter events, 3.7 us)
Async XLA Ops:
  6.5 78.5 %all-gather.5.cloned.1.call-start = ((), (), s32[]{:S(2)}) async-start(), calls=%async_computation.4 | async-start | bytes 4718592 | tf_op jit(solution)/shard_map/all_gather | solution.py:23
  7.3 114.9 %all-gather.7.cloned.1.call-start = ((), (), s32[]{:S(2)}) async-start(), calls=%async_computation.5 | async-start | bytes 2621440 | tf_op jit(solution)/shard_map/all_gather | solution.py:31
  7.3 80.8 %copy-start.5 = (f32[4096]{0:T(1024)S(1)}, f32[4096]{0:T(1024)}, u32[]{:S(2)}) copy-start(f32[4096]{0:T(1024)} %param.10) | copy-start | bytes 49156
  107.4 7.1 copy-start.4
  141.8 19.2 %copy-start.2 = (bf16[1,2048,4,128]{1,3,2,0:T(8,128)(2,1)S(1)}, bf16[1,2048,4,128]{1,3,2,0:T(8,128)(2,1)}, u32[]{:S(2)}) copy-start(bf16[1,2048,4,128]{1,3,2,0:T(8,128)(2,1)} %copy.49) | copy-start | bytes 6291460
  141.8 19.2 %copy-start.3 = (bf16[512,4,128]{0,2,1:T(8,128)(2,1)S(1)}, bf16[512,4,128]{0,2,1:T(8,128)(2,1)}, u32[]{:S(2)}) copy-start(bf16[512,4,128]{0,2,1:T(8,128)(2,1)} %copy.45) | copy-start | bytes 1572868
  198.0 19.2 %copy-start.1 = (bf16[1,2048,4,128]{1,3,2,0:T(8,128)(2,1)S(1)}, bf16[1,2048,4,128]{1,3,2,0:T(8,128)(2,1)}, u32[]{:S(2)}) copy-start(bf16[1,2048,4,128]{1,3,2,0:T(8,128)(2,1)} %copy.44) | copy-start | bytes 6291460
  247.0 14.4 %all-to-all-start.1 = ((f32[4,1,2048]{2,1,0:T(1,128)}), f32[4,1,2048]{2,1,0:T(1,128)S(1)}, u32[]{:S(2)}, u32[]{:S(2)}) async-start(f32[4,1,2048]{2,1,0:T(1,128)} %reshape.59), calls=%async_computation.1 | async-start | bytes 65536 | tf_op jit(solution)/shard_map/all_to_all | solution.py:66
  261.3 13.2 %all-to-all-start.2 = ((f32[4,1,2048]{2,1,0:T(1,128)}), f32[4,1,2048]{2,1,0:T(1,128)S(1)}, u32[]{:S(2)}, u32[]{:S(2)}) async-start(f32[4,1,2048]{2,1,0:T(1,128)} %reshape.61), calls=%async_computation.2 | async-start | bytes 65536 | tf_op jit(solution)/shard_map/all_to_all | solution.py:67
  274.5 53.1 %all-to-all-start = ((f32[1,2048,4,128]{3,2,0,1:T(4,128)}), f32[1,2048,4,128]{3,2,0,1:T(4,128)}, u32[]{:S(2)}, u32[]{:S(2)}) async-start(f32[1,2048,4,128]{3,2,0,1:T(4,128)} %copy.37), calls=%async_computation | async-start | bytes 8388608 | tf_op jit(solution)/shard_map/all_to_all | solution.py:68
  279.3 219.8 %all-reduce.2.cloned.1.call-start = ((), (), s32[]{:S(2)}) async-start(), calls=%async_computation.6 | async-start | bytes 8388608 | tf_op jit(solution)/shard_map/psum | solution.py:80
  332.9 5.3 copy-start
  342.7 297.3 %all-gather.9.cloned.1.call-start = ((), (), s32[]{:S(2)}) async-start(), calls=%async_computation.7 | async-start | bytes 28180480 | tf_op jit(solution)/shard_map/all_gather | solution.py:89
  343.2 372.8 %all-gather.11.cloned.1.call-start = ((), (), s32[]{:S(2)}) async-start(), calls=%async_computation.8 | async-start | bytes 14090240 | tf_op jit(solution)/shard_map/all_gather | solution.py:95
  343.8 296.1 %copy-start.6 = (f32[4096]{0:T(1024)S(1)}, f32[4096]{0:T(1024)}, u32[]{:S(2)}) copy-start(f32[4096]{0:T(1024)} %param.15) | copy-start | bytes 49156
  343.8 474.2 %reduce-scatter.2.cloned.1.call-start = ((), (), s32[]{:S(2)}) async-start(), calls=%async_computation.9 | async-start | bytes 4718592 | tf_op jit(solution)/shard_map/reduce_scatter | solution.py:98
Sparse Core Ops, SparseCore 0:
  9.5 75.5 all-gather.4
  101.0 21.0 all-gather.6
  342.8 156.3 all-reduce.1
  500.6 139.2 all-gather.8
  641.3 74.6 all-gather.10
  729.7 88.2 reduce-scatter.1
where the time goes:
time: 835 us; the launch traced here: 827 us
  waiting for transfers between devices  540 us (65%)
  matrix products  124 us (15%)
  other arithmetic  84.6 us (10%)
  local copies, waits for them, and re-layouts  52.2 us (6%)
  between operations  13.9 us (2%)
  starting transfers between devices  12.2 us (1%)
    psum x1, waiting for transfers between devices, per_device(): lax.psum(jnp.dot(attended, w_out, preferred_element_type=jnp.float32).ast...  155 us
    all_gather x1, waiting for transfers between devices, per_device(): lax.all_gather(w_gate_up, 'kv', axis=0, tiled=True)  132 us
    reduce_scatter x1, waiting for transfers between devices, per_device(): lax.psum_scatter(down_terms.astype(jnp.bfloat16), 'tp', scatter_dimension...  88.4 us
    all_gather x1, waiting for transfers between devices, per_device(): block_input = lax.all_gather(hidden_in, 'tp', axis=0, tiled=True)  65.3 us
    all_gather x1, waiting for transfers between devices, per_device(): lax.all_gather(w_down, 'kv', axis=1, tiled=True)  55.6 us
    all_to_all x1, waiting for transfers between devices, per_device(): lax.all_to_all(accum_all[None], 'kv', split_axis=1, concat_axis=0, tiled=...  42 us
    dot_general x2, matrix products, per_device(): jnp.einsum('qhd,khd->hqk', query_block, joined_key_rows, preferred_elemen...  38.7 us
    reduce_sum x2, other arithmetic, per_device(): masses.append(jnp.sum(raw_weights, axis=2).T)  38.4 us
  transfers between devices with their start and end apart: 9, of which 7 were waited for; matrix products, arithmetic and copies ran while one was open for 11% of the time, Pallas kernels for 0%

commit v1 on v0

--- a/solution.py
+++ b/solution.py
@@ -6,6 +6,18 @@
 
 EPSILON = 1e-05
 MASKED = -1e30
+
+
+def ring_product(x, axis, dim, term):
+    devices, index, width = (lax.axis_size(axis), lax.axis_index(axis), x.shape[dim])
+    ahead = [(i, (i + 1) % devices) for i in range(devices)]
+    block, total = (x, None)
+    for step in range(devices):
+        upcoming = lax.ppermute(block, axis, ahead) if step < devices - 1 else None
+        update = term(block, (index - step) % devices * width)
+        total = update if total is None else total + update
+        block = upcoming
+    return total
 
 
 def rms_scale(values_in, gain_vector):
@@ -83,11 +95,16 @@
     residual = block_input.astype(jnp.float32) + heads_sum
     mlp_in = rms_scale(residual, gain_mlp)
     residual_own = lax.dynamic_slice_in_dim(residual, tp_index * own_rows, own_rows, 0)
-    gate_up = jnp.einsum(
-        "td,dgf->tgf",
-        mlp_in,
-        lax.all_gather(w_gate_up, "kv", axis=0, tiled=True),
-        preferred_element_type=jnp.float32,
+    gate_up = ring_product(
+        w_gate_up,
+        "kv",
+        0,
+        lambda shard, start: jnp.einsum(
+            "td,dgf->tgf",
+            lax.dynamic_slice_in_dim(mlp_in, start, shard.shape[0], axis=1),
+            shard,
+            preferred_element_type=jnp.float32,
+        ),
     )
     activated = (jax.nn.silu(gate_up[:, 0, :]) * gate_up[:, 1, :]).astype(jnp.bfloat16)
     down_terms = jnp.dot(

time: 835 us -> 715 us (0.86)
  waiting for transfers between devices: 540 us -> 411 us
    ppermute x0 -> x3, waiting for transfers between devices: none -> 174 us  [ring_product(): upcoming = lax.ppermute(block, axis, ahead) if step < devices - 1 else None]
    all_gather x1 -> x0, waiting for transfers between devices: 132 us -> none  [per_device(): lax.all_gather(w_gate_up, 'kv', axis=0, tiled=True)]
    psum x1, waiting for transfers between devices: 155 us -> 29.1 us  [per_device(): lax.psum(jnp.dot(attended, w_out, preferred_element_type=jnp.float32).ast...]
    all_gather x1, waiting for transfers between devices: 55.6 us -> 9.54 us  [per_device(): lax.all_gather(w_down, 'kv', axis=1, tiled=True)]
    dot_general x1 -> x4, matrix products: 20.5 us -> 28.5 us  [per_device(): jnp.einsum('td,dgf->tgf', lax.dynamic_slice_in_dim(mlp_in, start, shard.s...]
    unnamed x25 -> x29, local copies, waits for them, and re-layouts: 28.1 us -> 28.1 us
  transfers between devices with their start and end apart: 9 -> 11, of which waited for: 7 -> 9; matrix products, arithmetic and copies ran while one was open for 11% -> 14% of each run, Pallas kernels for 0% -> 0%
where the time goes in v1:
time: 715 us; the launch traced here: 707 us
  waiting for transfers between devices  411 us (57%)
  matrix products  132 us (18%)
  other arithmetic  86.9 us (12%)
  local copies, waits for them, and re-layouts  52.3 us (7%)
  between operations  13.7 us (2%)
  starting transfers between devices  11.8 us (2%)
    ppermute x3, waiting for transfers between devices, ring_product(): upcoming = lax.ppermute(block, axis, ahead) if step < devices - 1 else None  174 us
    reduce_scatter x1, waiting for transfers between devices, per_device(): lax.psum_scatter(down_terms.astype(jnp.bfloat16), 'tp', scatter_dimension...  88.9 us
    all_gather x1, waiting for transfers between devices, per_device(): block_input = lax.all_gather(hidden_in, 'tp', axis=0, tiled=True)  65.3 us
    all_to_all x1, waiting for transfers between devices, per_device(): lax.all_to_all(accum_all[None], 'kv', split_axis=1, concat_axis=0, tiled=...  42.3 us
    reduce_sum x2, other arithmetic, per_device(): masses.append(jnp.sum(raw_weights, axis=2).T)  38.4 us
    dot_general x2, matrix products, per_device(): jnp.einsum('qhd,khd->hqk', query_block, joined_key_rows, preferred_elemen...  38.4 us
    dot_general x2, matrix products, per_device(): jnp.einsum('hqk,khd->qhd', raw_weights.astype(jnp.bfloat16), joined_value...  35.8 us
    psum x1, waiting for transfers between devices, per_device(): lax.psum(jnp.dot(attended, w_out, preferred_element_type=jnp.float32).ast...  29.1 us
  transfers between devices with their start and end apart: 11, of which 9 were waited for; matrix products, arithmetic and copies ran while one was open for 14% of the time, Pallas kernels for 0%

profile of v1, /device:TPU:0, one launch (start us, length us, event | category | flops | bytes accessed | tf_op | source)
XLA Modules:
  0.0 707.5 jit_solution(9438542337583224121)
XLA Ops:
  6.5 0.7 all-gather.4.cloned.1.call-update
  7.3 12.4 %copy.51 = bf16[512,8,4,384]{3,1,2,0:T(8,128)(2,1)} copy(bf16[512,8,4,384]{3,2,1,0:T(4,128)(2,1)} %bitcast.62) | data formatting | bytes 25165824
  19.7 65.3 %all-gather.4.cloned.1.call-done = bf16[512,4096]{1,0:T(8,128)(2,1)} async-done(((bf16[64,4096]{1,0:T(8,128)(2,1)}), bf16[512,4096]{1,0:T(8,128)(2,1)}) %all-gather.4.cloned.1.call-update) | async-done | bytes 4194320 | tf_op jit(solution)/shard_map/all_gather | solution.py:35
  85.0 3.1 fusion.12
  88.1 11.0 %fusion.19 = bf16[512,1536]{1,0:T(8,128)(2,1)S(1)} fusion(bf16[4096,1536]{1,0:T(8,128)(2,1)} %bitcast.63, bf16[512,4096]{1,0:T(8,128)(2,1)} %all-gather.4.cloned.1.call-done, f32[4096]{0:T(1024)S(1)} %copy-done.8, f32[512]{0:T(512)S(1)} %add_rsqrt_fusion.1), kind=kOutput, calls=%fused_computation.34 | convolution fusion | flops 6451625984 | bytes 18368512 | tf_op jit(solution)/shard_map/dot_general | solution.py:39
  100.0 0.9 copy.46
  100.9 6.4 fusion.71
  107.4 4.4 copy.44
  111.8 2.6 copy.49
  115.1 1.2 fusion.51
  116.4 4.2 copy_bitcast_fusion
  120.5 1.1 copy.45
  122.2 19.3 %fusion.1 = (f32[4,1024]{1,0:T(4,128)S(1)}, f32[4,1024,2560]{2,1,0:T(8,128)}) fusion(pred[2560]{0:T(1024)(128)(4,1)S(1)} %pad_add_fusion.1, bf16[512,4,128]{2,0,1:T(8,128)(2,1)S(1)} %copy.48, bf16[2048,4,128]{2,0,1:T(8,128)(2,1)} %get-tuple-element.26, bf16[2048,4,128]{2,0,1:T(8,128)(2,1)} %all-gather.6.cloned.1.call-done), kind=kOutput, calls=%fused_computation.5 | convolution fusion | flops 2721050624 | bytes 45632000 | tf_op jit(solution)/shard_map/qhd,khd->hqk/dot_general | solution.py:56
  141.5 19.2 %fusion.4 = f32[4,1024]{1,0:T(4,128)S(1)} fusion(f32[4,1024,2560]{2,1,0:T(8,128)} %get-tuple-element.19, f32[4,1024]{1,0:T(4,128)S(1)} %get-tuple-element.18, pred[2560]{0:T(1024)(128)(4,1)S(1)} %pad_add_fusion.1), kind=kLoop, calls=%fused_computation.8 | loop fusion | flops 52424704 | bytes 41978368 | tf_op jit(solution)/shard_map/reduce_sum | solution.py:65
  160.7 17.9 %fusion.33 = f32[1024,4,128]{0,2,1:T(8,128)} fusion(f32[4,1024,2560]{2,1,0:T(8,128)} %get-tuple-element.19, f32[4,1024]{1,0:T(4,128)S(1)} %get-tuple-element.18, pred[2560]{0:T(1024)(128)(4,1)S(1)} %pad_add_fusion.1, bf16[512,4,128]{0,2,1:T(8,128)(2,1)S(1)} %copy-done.5, bf16[2048,4,128]{0,2,1:T(8,128)(2,1)S(1)} %bitcast.71), kind=kOutput, calls=%fused_computation.48 | convolution fusion | flops 2742026240 | bytes 46680576 | tf_op jit(solution)/shard_map/hqk,khd->qhd/dot_general | solution.py:67
  178.6 19.1 %fusion = (f32[4,1024]{1,0:T(4,128)S(1)}, f32[4,1024,2560]{2,1,0:T(8,128)}) fusion(pred[2560]{0:T(1024)(128)(4,1)S(1)} %pad_add_fusion, bf16[512,4,128]{2,0,1:T(8,128)(2,1)S(1)} %copy.48, bf16[2048,4,128]{2,0,1:T(8,128)(2,1)S(1)} %get-tuple-element.27, bf16[2048,4,128]{2,0,1:T(8,128)(2,1)} %all-gather.6.cloned.1.call-done), kind=kOutput, calls=%fused_computation.4 | convolution fusion | flops 2721050624 | bytes 45632000 | tf_op jit(solution)/shard_map/qhd,khd->hqk/dot_general | solution.py:56
  197.7 19.2 %fusion.2 = f32[4,1024]{1,0:T(4,128)S(1)} fusion(f32[4,1024,2560]{2,1,0:T(8,128)} %get-tuple-element.21, f32[4,1024]{1,0:T(4,128)S(1)} %get-tuple-element.20, pred[2560]{0:T(1024)(128)(4,1)S(1)} %pad_add_fusion), kind=kLoop, calls=%fused_computation.6 | loop fusion | flops 52424704 | bytes 41978368 | tf_op jit(solution)/shard_map/reduce_sum | solution.py:65
  216.9 17.9 %fusion.30 = f32[1024,4,128]{0,2,1:T(8,128)} fusion(f32[4,1024,2560]{2,1,0:T(8,128)} %get-tuple-element.21, f32[4,1024]{1,0:T(4,128)S(1)} %get-tuple-element.20, pred[2560]{0:T(1024)(128)(4,1)S(1)} %pad_add_fusion, bf16[512,4,128]{0,2,1:T(8,128)(2,1)S(1)} %copy-done.5, bf16[2048,4,128]{0,2,1:T(8,128)(2,1)S(1)} %bitcast.70), kind=kOutput, calls=%fused_computation.47 | convolution fusion | flops 2742026240 | bytes 46680576 | tf_op jit(solution)/shard_map/hqk,khd->qhd/dot_general | solution.py:67
  235.7 9.7 %reduce.2 = f32[2048,4]{1,0:T(8,128)S(1)} reduce(f32[2048,1,4]{2,1,0:T(1,128)S(1)} %bitcast.66, f32[]{:T(128)} %broadcast.102), dimensions={1}, to_apply=%bitcast.50.reduce_sub_computation | reduce | bytes 65540
  245.5 1.3 reshape.62
  246.8 3.3 all-to-all-start.1
  250.5 9.3 %reduce = f32[2048,4]{1,0:T(8,128)S(1)} reduce(f32[2048,1,4]{2,1,0:T(1,128)S(1)} %bitcast.67, f32[]{:T(128)} %broadcast.102), dimensions={1}, to_apply=%bitcast.52.reduce_sub_computation | reduce | bytes 65540
  259.8 1.4 reshape.64
  261.2 3.3 all-to-all-start.2
  264.4 4.6 maximum_bitcast_fusion
  269.1 5.2 copy.37
  274.3 4.9 all-to-all-start
  280.1 1.7 reshape.63
  282.3 0.7 reduce.1
  283.0 1.7 reshape.65
  285.1 42.3 %all-to-all-done = f32[1,2048,4,128]{3,2,0,1:T(4,128)} async-done(((f32[1,2048,4,128]{3,2,0,1:T(4,128)}), f32[1,2048,4,128]{3,2,0,1:T(4,128)}, u32[]{:S(2)}, u32[]{:S(2)}) %all-to-all-start) | async-done | bytes 4194336 | tf_op jit(solution)/shard_map/all_to_all | solution.py:80
  327.4 5.3 copy.41
  332.7 5.1 multiply_reduce_fusion.1
  338.0 4.5 convolution_convert_fusion.1
  343.1 63.2 %collective-permute-done = bf16[1024,2,1376]{0,2,1:T(8,128)(2,1)} collective-permute-done((bf16[1024,2,1376]{0,2,1:T(8,128)(2,1)}, bf16[1024,2,1376]{0,2,1:T(8,128)(2,1)}, u32[]{:S(2)}, u32[]{:S(2)}) %collective-permute-start) | collective-permute-done | bytes 5636128 | tf_op jit(solution)/shard_map/ppermute | solution.py:16
  406.3 63.7 %collective-permute-done.1 = bf16[1024,2,1376]{0,2,1:T(8,128)(2,1)} collective-permute-done((bf16[1024,2,1376]{0,2,1:T(8,128)(2,1)}, bf16[1024,2,1376]{0,2,1:T(8,128)(2,1)}, u32[]{:S(2)}, u32[]{:S(2)}) %collective-permute-start.1) | collective-permute-done | bytes 5636128 | tf_op jit(solution)/shard_map/ppermute | solution.py:16
  470.0 29.1 %all-reduce.2.cloned.1.call-done = bf16[512,4096]{1,0:T(8,128)(2,1)} async-done(((bf16[512,4096]{1,0:T(8,128)(2,1)}), bf16[512,4096]{1,0:T(8,128)(2,1)}) %all-reduce.2.cloned.1.call-update) | async-done | bytes 4194320 | tf_op jit(solution)/shard_map/psum | solution.py:92
  499.0 8.9 %convert_add_fusion = (f32[512,4096]{1,0:T(8,128)}, f32[512]{0:T(512)S(1)}) fusion(bf16[512,4096]{1,0:T(8,128)(2,1)} %all-gather.4.cloned.1.call-done, bf16[512,4096]{1,0:T(8,128)(2,1)} %all-reduce.2.cloned.1.call-done), kind=kLoop, calls=%fused_computation.14 | loop fusion | flops 10485248 | bytes 16779264 | tf_op jit(solution)/shard_map/add | solution.py:95
  508.0 2.4 multiply_convert_fusion
  510.4 6.3 fusion.45
  516.7 5.3 fusion.41
  522.0 7.7 %fusion.43 = f32[512,2,1376]{0,2,1:T(8,128)} fusion(bf16[1024,2,1376]{0,2,1:T(8,128)(2,1)} %collective-permute-done, bf16[512,4096]{1,0:T(8,128)(2,1)S(1)} %multiply_convert_fusion, s32[]{:T(128)S(6)} %select_n.61), kind=kOutput, calls=%fused_computation.55 | convolution fusion | flops 2885681152 | bytes 12320772 | tf_op jit(solution)/shard_map/td,dgf->tgf/dot_general | solution.py:102
  529.7 47.4 %collective-permute-done.2 = bf16[1024,2,1376]{0,2,1:T(8,128)(2,1)} collective-permute-done((bf16[1024,2,1376]{0,2,1:T(8,128)(2,1)}, bf16[1024,2,1376]{0,2,1:T(8,128)(2,1)}, u32[]{:S(2)}, u32[]{:S(2)}) %collective-permute-start.2) | collective-permute-done | bytes 5636128 | tf_op jit(solution)/shard_map/ppermute | solution.py:16
  577.1 9.3 %add_add_fusion = f32[512,2,1376]{0,2,1:T(8,128)} fusion(f32[512,2,1376]{0,2,1:T(8,128)S(1)} %fusion.41, f32[512,2,1376]{0,2,1:T(8,128)S(1)} %fusion.45, f32[512,2,1376]{0,2,1:T(8,128)} %fusion.43, bf16[1024,2,1376]{0,2,1:T(8,128)(2,1)} %collective-permute-done.2, bf16[512,4096]{1,0:T(8,128)(2,1)S(1)} %multiply_convert_fusion, s32[]{:T(128)S(6)} %select_n.65), kind=kOutput, calls=%fused_computation.24 | convolution fusion | flops 2889908224 | bytes 29229060 | tf_op jit(solution)/shard_map/td,dgf->tgf/dot_general | solution.py:102
  586.3 9.5 %all-gather.8.cloned.1.call-done = bf16[1376,4096]{1,0:T(8,128)(2,1)} async-done(((bf16[1376,1024]{1,0:T(8,128)(2,1)}), bf16[1376,4096]{1,0:T(8,128)(2,1)}) %all-gather.8.cloned.1.call-update) | async-done | bytes 11272208 | tf_op jit(solution)/shard_map/all_gather | solution.py:112
  595.9 13.7 %convolution_convert_fusion = bf16[512,4096]{1,0:T(8,128)(2,1)} fusion(bf16[1376,4096]{1,0:T(8,128)(2,1)} %all-gather.8.cloned.1.call-done, f32[512,2,1376]{0,2,1:T(8,128)} %add_add_fusion), kind=kOutput, calls=%fused_computation.22 | convolution fusion | flops 5777686528 | bytes 21102592 | tf_op jit(solution)/shard_map/dot_general | solution.py:110
  609.6 88.9 %reduce-scatter.2.cloned.1.call-done = bf16[64,4096]{1,0:T(8,128)(2,1)} async-done(((bf16[512,4096]{1,0:T(8,128)(2,1)}), bf16[64,4096]{1,0:T(8,128)(2,1)}) %reduce-scatter.2.cloned.1.call-update) | async-done | bytes 524304 | tf_op jit(solution)/shard_map/reduce_scatter | solution.py:115
  698.5 2.3 add_convert_fusion
  (54 shorter events, 6.1 us)
Async XLA Ops:
  6.5 78.5 %all-gather.4.cloned.1.call-start = ((), (), s32[]{:S(2)}) async-start(), calls=%async_computation.4 | async-start | bytes 4718592 | tf_op jit(solution)/shard_map/all_gather | solution.py:35
  7.3 114.9 %all-gather.6.cloned.1.call-start = ((), (), s32[]{:S(2)}) async-start(), calls=%async_computation.5 | async-start | bytes 2621440 | tf_op jit(solution)/shard_map/all_gather | solution.py:43
  7.3 80.8 %copy-start.8 = (f32[4096]{0:T(1024)S(1)}, f32[4096]{0:T(1024)}, u32[]{:S(2)}) copy-start(f32[4096]{0:T(1024)} %param.10) | copy-start | bytes 49156
  107.4 7.1 %copy-start.7 = (s32[2]{0:T(128)S(1)}, s32[2]{0:T(128)}, u32[]{:S(2)}) copy-start(s32[2]{0:T(128)} %param.13) | copy-start | bytes 28
  141.5 19.2 %copy-start.4 = (bf16[1,2048,4,128]{1,3,2,0:T(8,128)(2,1)S(1)}, bf16[1,2048,4,128]{1,3,2,0:T(8,128)(2,1)}, u32[]{:S(2)}) copy-start(bf16[1,2048,4,128]{1,3,2,0:T(8,128)(2,1)} %copy.49) | copy-start | bytes 6291460
  141.5 19.2 %copy-start.5 = (bf16[512,4,128]{0,2,1:T(8,128)(2,1)S(1)}, bf16[512,4,128]{0,2,1:T(8,128)(2,1)}, u32[]{:S(2)}) copy-start(bf16[512,4,128]{0,2,1:T(8,128)(2,1)} %copy.45) | copy-start | bytes 1572868
  197.7 19.2 %copy-start.3 = (bf16[1,2048,4,128]{1,3,2,0:T(8,128)(2,1)S(1)}, bf16[1,2048,4,128]{1,3,2,0:T(8,128)(2,1)}, u32[]{:S(2)}) copy-start(bf16[1,2048,4,128]{1,3,2,0:T(8,128)(2,1)} %copy.44) | copy-start | bytes 6291460
  246.8 14.3 %all-to-all-start.1 = ((f32[4,1,2048]{2,1,0:T(1,128)}), f32[4,1,2048]{2,1,0:T(1,128)S(1)}, u32[]{:S(2)}, u32[]{:S(2)}) async-start(f32[4,1,2048]{2,1,0:T(1,128)} %reshape.62), calls=%async_computation.1 | async-start | bytes 65536 | tf_op jit(solution)/shard_map/all_to_all | solution.py:78
  261.2 13.2 %all-to-all-start.2 = ((f32[4,1,2048]{2,1,0:T(1,128)}), f32[4,1,2048]{2,1,0:T(1,128)S(1)}, u32[]{:S(2)}, u32[]{:S(2)}) async-start(f32[4,1,2048]{2,1,0:T(1,128)} %reshape.64), calls=%async_computation.2 | async-start | bytes 65536 | tf_op jit(solution)/shard_map/all_to_all | solution.py:79
  274.3 53.1 %all-to-all-start = ((f32[1,2048,4,128]{3,2,0,1:T(4,128)}), f32[1,2048,4,128]{3,2,0,1:T(4,128)}, u32[]{:S(2)}, u32[]{:S(2)}) async-start(f32[1,2048,4,128]{3,2,0,1:T(4,128)} %copy.37), calls=%async_computation | async-start | bytes 8388608 | tf_op jit(solution)/shard_map/all_to_all | solution.py:80
  279.2 219.9 %all-reduce.2.cloned.1.call-start = ((), (), s32[]{:S(2)}) async-start(), calls=%async_computation.6 | async-start | bytes 8388608 | tf_op jit(solution)/shard_map/psum | solution.py:92
  332.7 5.3 copy-start.2
  342.5 253.4 %all-gather.8.cloned.1.call-start = ((), (), s32[]{:S(2)}) async-start(), calls=%async_computation.7 | async-start | bytes 14090240 | tf_op jit(solution)/shard_map/all_gather | solution.py:112
  342.5 63.7 %collective-permute-start = (bf16[1024,2,1376]{0,2,1:T(8,128)(2,1)}, bf16[1024,2,1376]{0,2,1:T(8,128)(2,1)}, u32[]{:S(2)}, u32[]{:S(2)}) collective-permute-start(bf16[1024,2,1376]{0,2,1:T(8,128)(2,1)} %param.16), channel_id=1, source_target_pairs={{0,1},{1,2},{2,3},{3,0},{4,5},{5,6},{6,7},{7,4},{8,9},{9,10},{10,1... | collective-permute-start | bytes 16908296 | tf_op jit(solution)/shard_map/ppermute | solution.py:16
  343.1 355.4 %reduce-scatter.2.cloned.1.call-start = ((), (), s32[]{:S(2)}) async-start(), calls=%async_computation.8 | async-start | bytes 4718592 | tf_op jit(solution)/shard_map/reduce_scatter | solution.py:115
  406.3 63.7 %collective-permute-start.1 = (bf16[1024,2,1376]{0,2,1:T(8,128)(2,1)}, bf16[1024,2,1376]{0,2,1:T(8,128)(2,1)}, u32[]{:S(2)}, u32[]{:S(2)}) collective-permute-start(bf16[1024,2,1376]{0,2,1:T(8,128)(2,1)} %collective-permute-done), channel_id=1, source_target_pairs={{0,1},{1,2},{2,3},{3,0},{4,5},{5,6},{6,7},{7,4},{8,9},{9,10},{10,1... | collective-permute-start | bytes 16908296 | tf_op jit(solution)/shard_map/ppermute | solution.py:16
  470.0 107.1 %collective-permute-start.2 = (bf16[1024,2,1376]{0,2,1:T(8,128)(2,1)}, bf16[1024,2,1376]{0,2,1:T(8,128)(2,1)}, u32[]{:S(2)}, u32[]{:S(2)}) collective-permute-start(bf16[1024,2,1376]{0,2,1:T(8,128)(2,1)} %collective-permute-done.1), channel_id=1, source_target_pairs={{0,1},{1,2},{2,3},{3,0},{4,5},{5,6},{6,7},{7,4},{8,9},{9,10},{10,1... | collective-permute-start | bytes 16908296 | tf_op jit(solution)/shard_map/ppermute | solution.py:16
  470.0 38.0 %copy-start.6 = (f32[4096]{0:T(1024)S(1)}, f32[4096]{0:T(1024)}, u32[]{:S(2)}) copy-start(f32[4096]{0:T(1024)} %param.15) | copy-start | bytes 49156
  499.0 9.0 %copy-start = (bf16[512,4096]{1,0:T(8,128)(2,1)S(1)}, bf16[512,4096]{1,0:T(8,128)(2,1)}, u32[]{:S(2)}) copy-start(bf16[512,4096]{1,0:T(8,128)(2,1)} %all-gather.4.cloned.1.call-done) | copy-start | bytes 12582916
  499.0 9.0 %copy-start.1 = (bf16[512,4096]{1,0:T(8,128)(2,1)S(1)}, bf16[512,4096]{1,0:T(8,128)(2,1)}, u32[]{:S(2)}) copy-start(bf16[512,4096]{1,0:T(8,128)(2,1)} %all-reduce.2.cloned.1.call-done) | copy-start | bytes 12582916
Sparse Core Ops, SparseCore 0:
  9.5 75.5 all-gather.3
  101.0 21.0 all-gather.5
  342.6 156.3 all-reduce.1
  500.5 95.3 all-gather.7
  609.7 88.7 reduce-scatter.1
